TPU v7x, 32 devices: a whole 2x2x4 slice. The times are simulated.
32 devices in a mesh: tm: 8 (over z, y), space: 4 (over x, core).
Axes of the slice: x: 2, y: 2, z: 4, core: 2. Of those that a mesh axis runs over, the one named last changes fastest.
Arguments:
- initial: float32 [8, 128, 128], P('space'), may hold values from -6 to 6
- start_guess: float32 [8, 8, 128, 128], P('tm', 'space'), may hold values from -6 to 6
- forcing: float32 [8, 5, 8, 128, 128], P('tm', None, 'space'), may hold values from -6 to 6
- step_size: float32 [8], P('tm'), may hold values from 0.06 to 0.16
Outputs:
- fine_values: float32 [8, 5, 8, 128, 128], P('tm', None, 'space')
All inputs are finite; a program needn't handle non-finite values.
Results may differ from a plain program's by a relative error of at most 0.0001.
Values sent between devices are 32-bit elements; how exact they have to be, the bound alone decides.
A program may use at most 64 MiB of HBM per device.

v0:
```python
import math

import jax
import jax.numpy as jnp
import numpy as np
from jax import lax
from jax.sharding import PartitionSpec as P

ITERS = 2


def with_halo(block, sides, width):
    for axis, dim in sides:
        count = lax.axis_size(axis)
        forward = [(i, i + 1) for i in range(count - 1)]
        backward = [(target, source) for source, target in forward]
        low = lax.ppermute(
            lax.slice_in_dim(block, block.shape[dim] - width, None, axis=dim), axis, forward
        )
        high = lax.ppermute(lax.slice_in_dim(block, 0, width, axis=dim), axis, backward)
        block = jnp.concatenate([low, block, high], axis=dim)
    return block


def shifted(value, axis, steps):
    count = lax.axis_size(axis)
    first, last = (max(0, -steps), min(count, count - steps))
    return lax.ppermute(value, axis, [(source, source + steps) for source in range(first, last)])


def prefix(part, axis, combine, identity):
    place = lax.axis_index(axis)
    gathered = jax.tree.map(lambda a: lax.all_gather(a, axis), part)
    state = jax.tree.map(lambda a, e: jnp.zeros_like(a) + jnp.asarray(e, a.dtype), part, identity)

    def one(step, state):
        return combine(
            state, jax.tree.map(lambda a: lax.dynamic_index_in_dim(a, step, 0, False), gathered)
        )

    return lax.fori_loop(0, place, one, state)


def node_tables():
    radical = math.sqrt(3.0 / 7.0)
    node_times = [0.0, (1.0 - radical) / 2.0, 0.5, (1.0 + radical) / 2.0, 1.0]
    integrals = np.zeros((4, 5))
    for column in range(5):
        coeffs = [1.0]
        for other_index in range(5):
            if other_index == column:
                continue
            other_time = node_times[other_index]
            scaling = node_times[column] - other_time
            grown = [0.0] * (len(coeffs) + 1)
            for exponent in range(len(coeffs)):
                grown[exponent + 1] += coeffs[exponent] / scaling
                grown[exponent] -= coeffs[exponent] * other_time / scaling
            coeffs = grown
        for section in range(4):
            integrals[section, column] = sum(
                (
                    coeffs[exponent]
                    * (
                        node_times[section + 1] ** (exponent + 1)
                        - node_times[section] ** (exponent + 1)
                    )
                    / (exponent + 1)
                    for exponent in range(len(coeffs))
                )
            )
    coarse = [0.0, 0.5, 1.0]
    interp = np.zeros((5, 3))
    for column in range(3):
        for section in range(5):
            weight = 1.0
            for other_index in range(3):
                if other_index != column:
                    weight = (
                        weight
                        * (node_times[section] - coarse[other_index])
                        / (coarse[column] - coarse[other_index])
                    )
            interp[section, column] = weight
    return (np.array(node_times), integrals, interp)


def stencil(padded):
    center = padded[..., 1:-1, :, :]
    widths = [(0, 0)] * (center.ndim - 2) + [(1, 1), (1, 1)]
    framed = jnp.pad(center, widths)
    return (
        padded[..., 2:, :, :]
        + padded[..., :-2, :, :]
        + framed[..., 2:, 1:-1]
        + framed[..., :-2, 1:-1]
        + framed[..., 1:-1, 2:]
        + framed[..., 1:-1, :-2]
        - 6.0 * center
    )


def laplace_one(field):
    return stencil(with_halo(field, (("space", 0),), 1))


def laplace_nodes(fields):
    return stencil(with_halo(fields, (("space", 1),), 1))


def sine_matrix(length, row_first, row_count, col_count):
    rows = jnp.arange(row_count, dtype=jnp.int32) + row_first + 1
    columns = jnp.arange(col_count, dtype=jnp.int32) + 1
    phase = rows[:, None] * columns[None, :] % (2 * (length + 1))
    return math.sqrt(2.0 / (length + 1)) * jnp.sin(
        math.pi / (length + 1) * phase.astype(jnp.float32)
    )


def eigen_weights(length, first, count):
    indices = (jnp.arange(count, dtype=jnp.int32) + first + 1).astype(jnp.float32)
    return 2.0 - 2.0 * jnp.cos(math.pi / (length + 1) * indices)


def compose(earlier, later):
    return (earlier[0] * later[0], later[0] * earlier[1] + later[1])


def body(initial, start_guess, forcing, step_size):
    depth, width_x, width_y = initial.shape
    length_z = depth * lax.axis_size("space")
    z_first = lax.axis_index("space") * depth
    position = lax.axis_index("tm")
    highest = lax.Precision.HIGHEST
    x_matrix = sine_matrix(width_x, 0, width_x, width_x)
    y_matrix = sine_matrix(width_y, 0, width_y, width_y)
    eigen = (
        eigen_weights(length_z, z_first, depth)[:, None, None]
        + eigen_weights(width_x, 0, width_x)[None, :, None]
        + eigen_weights(width_y, 0, width_y)[None, None, :]
    )

    def lateral(field):
        mixed = jnp.einsum("ai,zij->zaj", x_matrix, field, precision=highest)
        return jnp.einsum("zaj,bj->zab", mixed, y_matrix, precision=highest)

    def forward(field):
        flat = lateral(field).reshape(depth, width_x * width_y)
        shard_rows = lax.all_gather(flat, "space", axis=0, tiled=True)
        spectral = jnp.zeros_like(flat) + jnp.dot(
            sine_matrix(length_z, z_first, depth, shard_rows.shape[0]),
            shard_rows,
            precision=highest,
            preferred_element_type=jnp.float32,
        )
        return spectral.reshape(depth, width_x, width_y)

    node_times, integrals, interp = node_tables()
    full_step = step_size[0]
    half_step = 0.5 * full_step
    initial_hat = forward(initial)
    values = jnp.broadcast_to(start_guess[0][None], (5, depth, width_x, width_y))
    for sweep_round in range(ITERS):
        previous = shifted(values[4], "tm", 1)
        values = values.at[0].set(jnp.where(position == 0, initial, previous))
        lap_old = laplace_nodes(values)
        rates = lap_old + forcing[0]
        swept = [values[0]]
        lap_new = [lap_old[0]]
        for section in range(4):
            quadrature = sum(
                (float(integrals[section, column]) * rates[column] for column in range(5))
            )
            spacing = float(node_times[section + 1] - node_times[section])
            advanced = (
                swept[section]
                + full_step * spacing * (lap_new[section] - lap_old[section])
                + full_step * quadrature
            )
            swept.append(advanced)
            lap_new.append(laplace_one(advanced))
        new_rates = [lap_new[column] + forcing[0, column] for column in range(5)]
        first_half = full_step * sum(
            (
                float(integrals[0, column] + integrals[1, column]) * new_rates[column]
                for column in range(5)
            )
        )
        second_half = full_step * sum(
            (
                float(integrals[2, column] + integrals[3, column]) * new_rates[column]
                for column in range(5)
            )
        )
        left = first_half - half_step * lap_new[0]
        right = second_half - half_step * lap_new[2]
        forced = left + half_step * laplace_one(left) + right
        forced_hat = forward(forced)
        factor = 1.0 - half_step * eigen
        prefix_gain, prefix_sum = prefix(
            (factor * factor, forced_hat),
            "tm",
            compose,
            (jnp.ones_like(eigen), jnp.zeros_like(eigen)),
        )
        inverse_flat = (prefix_gain * initial_hat + prefix_sum).reshape(depth, width_x * width_y)
        accumulate_shard_rows = lax.all_gather(inverse_flat, "space", axis=0, tiled=True)
        physical = jnp.zeros_like(inverse_flat) + jnp.dot(
            sine_matrix(length_z, z_first, depth, accumulate_shard_rows.shape[0]),
            accumulate_shard_rows,
            precision=highest,
            preferred_element_type=jnp.float32,
        )
        coarse_first = lateral(physical.reshape(depth, width_x, width_y))
        coarse_middle = coarse_first + half_step * laplace_one(coarse_first) + left
        coarse_ending = coarse_middle + half_step * laplace_one(coarse_middle) + right
        deltas = [coarse_first - swept[0], coarse_middle - swept[2], coarse_ending - swept[4]]
        values = jnp.stack(
            [
                swept[section]
                + sum((float(interp[section, column]) * deltas[column] for column in range(3)))
                for section in range(5)
            ]
        )
    return values[None]


def solution(mesh):
    in_specs = (
        P("space", None, None),
        P("tm", "space", None, None),
        P("tm", None, "space", None, None),
        P("tm"),
    )
    out_specs = P("tm", None, "space", None, None)
    return jax.shard_map(body, mesh=mesh, in_specs=in_specs, out_specs=out_specs, check_vma=False)
```

profile of v0, /device:TPU:30, one launch (start us, length us, event | category | flops | bytes accessed | tf_op | source)
XLA Modules:
  0.0 293.3 jit_solution(4274129726435221056)
XLA Ops:
  8.5 5.3 %collective-permute-done = f32[2,128,128]{2,1,0:T(8,128)S(1)} collective-permute-done((f32[2,128,128]{2,1,0:T(8,128)}, f32[2,128,128]{2,1,0:T(8,128)S(1)}, u32[]{:S(2)}, u32[]{:S(2)}) %collective-permute-start) | collective-permute-done | bytes 131104 | tf_op jit(solution)/shard_map/ppermute | solution.py:28
  17.0 2.4 collective-permute-start.2
  21.6 3.8 %collective-permute-done.2 = f32[5,1,128,128]{3,2,1,0:T(8,128)S(1)} collective-permute-done((f32[5,1,128,128]{3,2,1,0:T(8,128)S(1)}, f32[5,1,128,128]{3,2,1,0:T(8,128)S(1)}, u32[]{:S(2)}, u32[]{:S(2)}) %collective-permute-start.2) | collective-permute-done | bytes 327712 | tf_op jit(solution)/shard_map/ppermute | solution.py:17
  38.0 3.2 %collective-permute-done.6 = f32[1,128,128]{2,1,0:T(8,128)S(1)} collective-permute-done((f32[1,128,128]{2,1,0:T(8,128)S(1)}, f32[1,128,128]{2,1,0:T(8,128)S(1)}, u32[]{:S(2)}, u32[]{:S(2)}) %collective-permute-start.6) | collective-permute-done | bytes 65568 | tf_op jit(solution)/shard_map/ppermute | solution.py:17
  45.6 3.1 %collective-permute-done.8 = f32[1,128,128]{2,1,0:T(8,128)S(1)} collective-permute-done((f32[1,128,128]{2,1,0:T(8,128)S(1)}, f32[1,128,128]{2,1,0:T(8,128)S(1)}, u32[]{:S(2)}, u32[]{:S(2)}) %collective-permute-start.8) | collective-permute-done | bytes 65568 | tf_op jit(solution)/shard_map/ppermute | solution.py:17
  50.9 3.6 %collective-permute-start.9 = (f32[1,128,128]{2,1,0:T(8,128)S(1)}, f32[1,128,128]{2,1,0:T(8,128)S(1)}, u32[]{:S(2)}, u32[]{:S(2)}) collective-permute-start(f32[1,128,128]{2,1,0:T(8,128)S(1)} %get-tuple-element.187), channel_id=1, source_target_pairs={{1,0},{2,1},{3,2},{5,4},{6,5},{7,6},{9,8},{10,9},{11,10},{13,12},{... | collective-permute-start | bytes 196616 | tf_op jit(solution)/shard_map/ppermute | solution.py:20
  56.6 3.7 %collective-permute-start.11 = (f32[1,128,128]{2,1,0:T(8,128)S(1)}, f32[1,128,128]{2,1,0:T(8,128)S(1)}, u32[]{:S(2)}, u32[]{:S(2)}) collective-permute-start(f32[1,128,128]{2,1,0:T(8,128)S(1)} %get-tuple-element.185), channel_id=1, source_target_pairs={{1,0},{2,1},{3,2},{5,4},{6,5},{7,6},{9,8},{10,9},{11,10},{13,12},{... | collective-permute-start | bytes 196616 | tf_op jit(solution)/shard_map/ppermute | solution.py:20
  62.3 3.6 %collective-permute-done.12 = f32[1,128,128]{2,1,0:T(8,128)S(1)} collective-permute-done((f32[1,128,128]{2,1,0:T(8,128)S(1)}, f32[1,128,128]{2,1,0:T(8,128)S(1)}, u32[]{:S(2)}, u32[]{:S(2)}) %collective-permute-start.12) | collective-permute-done | bytes 65568 | tf_op jit(solution)/shard_map/ppermute | solution.py:17
  67.2 6.5 %all-gather = f32[4,2,16384]{2,1,0:T(2,128)S(1)} all-gather(f32[1,2,16384]{2,1,0:T(2,128)S(1)} %reshape.313), channel_id=1, replica_groups=mesh['tm'=8,'space'=4] {'space'}, dimensions={0}, use_global_device_ids=true | all-gather | bytes 655360 | tf_op jit(solution)/shard_map/all_gather | solution.py:149
  76.8 7.3 %all-gather.1 = f32[4,2,16384]{2,1,0:T(2,128)S(1)} all-gather(f32[1,2,16384]{2,1,0:T(2,128)S(1)} %reshape.315), channel_id=1, replica_groups=mesh['tm'=8,'space'=4] {'space'}, dimensions={0}, use_global_device_ids=true | all-gather | bytes 655360 | tf_op jit(solution)/shard_map/all_gather | solution.py:149
  85.2 29.8 %all-gather.11.cloned.1.call-done = f32[8,2,128,128]{3,2,1,0:T(8,128)} async-done(((f32[1,2,128,128]{3,2,1,0:T(8,128)}), f32[8,2,128,128]{3,2,1,0:T(8,128)}) %all-gather.11.cloned.1.call-update) | async-done | bytes 1048592 | tf_op jit(solution)/shard_map/all_gather | solution.py:33
  115.0 7.5 %while.26 = (s32[]{:T(128)}, f32[2,128,128]{2,1,0:T(8,128)S(1)}, f32[2,128,128]{2,1,0:T(8,128)S(1)}, s32[]{:T(128)}, f32[8,2,128,128]{3,2,1,0:T(8,128)}, /*index...) while((s32[]{:T(128)}, f32[2,128,128]{2,1,0:T(8,128)S(1)}, f32[2,128,128]{2,1,0:T(8,128)S(1)}, ...), condition=%wide.region_1.2_spmd, body=%wide.region_0.1_spmd.sunk | while | flops 98309 | bytes 786563 | solution.py:41
  122.6 6.5 %all-gather.2 = f32[4,2,16384]{2,1,0:T(2,128)S(1)} all-gather(f32[1,2,16384]{2,1,0:T(2,128)S(1)} %reshape.317), channel_id=1, replica_groups=mesh['tm'=8,'space'=4] {'space'}, dimensions={0}, use_global_device_ids=true | all-gather | bytes 655360 | tf_op jit(solution)/shard_map/all_gather | solution.py:207
  131.4 3.1 %collective-permute-start.13 = (f32[1,128,128]{2,1,0:T(8,128)S(1)}, f32[1,128,128]{2,1,0:T(8,128)S(1)}, u32[]{:S(2)}, u32[]{:S(2)}) collective-permute-start(f32[1,128,128]{2,1,0:T(8,128)S(1)} %get-tuple-element.183), channel_id=1, source_target_pairs={{1,0},{2,1},{3,2},{5,4},{6,5},{7,6},{9,8},{10,9},{11,10},{13,12},{... | collective-permute-start | bytes 196616 | tf_op jit(solution)/shard_map/ppermute | solution.py:20
  136.4 3.6 %collective-permute-done.14 = f32[1,128,128]{2,1,0:T(8,128)S(1)} collective-permute-done((f32[1,128,128]{2,1,0:T(8,128)S(1)}, f32[1,128,128]{2,1,0:T(8,128)S(1)}, u32[]{:S(2)}, u32[]{:S(2)}) %collective-permute-start.14) | collective-permute-done | bytes 65568 | tf_op jit(solution)/shard_map/ppermute | solution.py:17
  144.6 3.2 %collective-permute-done.16 = f32[1,128,128]{2,1,0:T(8,128)S(1)} collective-permute-done((f32[1,128,128]{2,1,0:T(8,128)S(1)}, f32[1,128,128]{2,1,0:T(8,128)S(1)}, u32[]{:S(2)}, u32[]{:S(2)}) %collective-permute-start.16) | collective-permute-done | bytes 65568 | tf_op jit(solution)/shard_map/ppermute | solution.py:17
  149.4 5.6 %collective-permute-done.17 = f32[2,128,128]{2,1,0:T(8,128)S(1)} collective-permute-done((f32[2,128,128]{2,1,0:T(8,128)S(1)}, f32[2,128,128]{2,1,0:T(8,128)S(1)}, u32[]{:S(2)}, u32[]{:S(2)}) %collective-permute-start.17) | collective-permute-done | bytes 131104 | tf_op jit(solution)/shard_map/ppermute | solution.py:28
  156.9 2.4 collective-permute-start.19
  161.5 3.8 %collective-permute-done.19 = f32[5,1,128,128]{3,2,1,0:T(8,128)S(1)} collective-permute-done((f32[5,1,128,128]{3,2,1,0:T(8,128)S(1)}, f32[5,1,128,128]{3,2,1,0:T(8,128)S(1)}, u32[]{:S(2)}, u32[]{:S(2)}) %collective-permute-start.19) | collective-permute-done | bytes 327712 | tf_op jit(solution)/shard_map/ppermute | solution.py:17
  170.2 3.2 %collective-permute-done.21 = f32[1,128,128]{2,1,0:T(8,128)S(1)} collective-permute-done((f32[1,128,128]{2,1,0:T(8,128)S(1)}, f32[1,128,128]{2,1,0:T(8,128)S(1)}, u32[]{:S(2)}, u32[]{:S(2)}) %collective-permute-start.21) | collective-permute-done | bytes 65568 | tf_op jit(solution)/shard_map/ppermute | solution.py:17
  175.5 2.6 collective-permute-start.23
  178.1 3.0 %collective-permute-done.23 = f32[1,128,128]{2,1,0:T(8,128)S(1)} collective-permute-done((f32[1,128,128]{2,1,0:T(8,128)S(1)}, f32[1,128,128]{2,1,0:T(8,128)S(1)}, u32[]{:S(2)}, u32[]{:S(2)}) %collective-permute-start.23) | collective-permute-done | bytes 65568 | tf_op jit(solution)/shard_map/ppermute | solution.py:17
  185.6 3.2 %collective-permute-done.25 = f32[1,128,128]{2,1,0:T(8,128)S(1)} collective-permute-done((f32[1,128,128]{2,1,0:T(8,128)S(1)}, f32[1,128,128]{2,1,0:T(8,128)S(1)}, u32[]{:S(2)}, u32[]{:S(2)}) %collective-permute-start.25) | collective-permute-done | bytes 65568 | tf_op jit(solution)/shard_map/ppermute | solution.py:17
  193.2 3.2 %collective-permute-done.27 = f32[1,128,128]{2,1,0:T(8,128)S(1)} collective-permute-done((f32[1,128,128]{2,1,0:T(8,128)S(1)}, f32[1,128,128]{2,1,0:T(8,128)S(1)}, u32[]{:S(2)}, u32[]{:S(2)}) %collective-permute-start.27) | collective-permute-done | bytes 65568 | tf_op jit(solution)/shard_map/ppermute | solution.py:17
  201.0 3.1 %collective-permute-done.29 = f32[1,128,128]{2,1,0:T(8,128)S(1)} collective-permute-done((f32[1,128,128]{2,1,0:T(8,128)S(1)}, f32[1,128,128]{2,1,0:T(8,128)S(1)}, u32[]{:S(2)}, u32[]{:S(2)}) %collective-permute-start.29) | collective-permute-done | bytes 65568 | tf_op jit(solution)/shard_map/ppermute | solution.py:17
  205.4 6.5 %all-gather.3 = f32[4,2,16384]{2,1,0:T(2,128)S(1)} all-gather(f32[1,2,16384]{2,1,0:T(2,128)S(1)} %reshape.319), channel_id=1, replica_groups=mesh['tm'=8,'space'=4] {'space'}, dimensions={0}, use_global_device_ids=true | all-gather | bytes 655360 | tf_op jit(solution)/shard_map/all_gather | solution.py:149
  213.7 39.1 %all-gather.13.cloned.1.call-done = f32[8,2,128,128]{3,2,1,0:T(8,128)} async-done(((f32[1,2,128,128]{3,2,1,0:T(8,128)}), f32[8,2,128,128]{3,2,1,0:T(8,128)}) %all-gather.13.cloned.1.call-update) | async-done | bytes 1048592 | tf_op jit(solution)/shard_map/all_gather | solution.py:33
  252.8 7.5 %while.27 = (s32[]{:T(128)}, f32[2,128,128]{2,1,0:T(8,128)S(1)}, f32[2,128,128]{2,1,0:T(8,128)S(1)}, s32[]{:T(128)}, f32[8,2,128,128]{3,2,1,0:T(8,128)}, /*index...) while((s32[]{:T(128)}, f32[2,128,128]{2,1,0:T(8,128)S(1)}, f32[2,128,128]{2,1,0:T(8,128)S(1)}, ...), condition=%wide.region_3.4_spmd, body=%wide.region_2.3_spmd.sunk | while | flops 98309 | bytes 786563 | solution.py:41
  260.5 6.5 %all-gather.4 = f32[4,2,16384]{2,1,0:T(2,128)S(1)} all-gather(f32[1,2,16384]{2,1,0:T(2,128)S(1)} %reshape.321), channel_id=1, replica_groups=mesh['tm'=8,'space'=4] {'space'}, dimensions={0}, use_global_device_ids=true | all-gather | bytes 655360 | tf_op jit(solution)/shard_map/all_gather | solution.py:207
  269.3 3.1 %collective-permute-start.30 = (f32[1,128,128]{2,1,0:T(8,128)S(1)}, f32[1,128,128]{2,1,0:T(8,128)S(1)}, u32[]{:S(2)}, u32[]{:S(2)}) collective-permute-start(f32[1,128,128]{2,1,0:T(8,128)S(1)} %get-tuple-element.169), channel_id=1, source_target_pairs={{1,0},{2,1},{3,2},{5,4},{6,5},{7,6},{9,8},{10,9},{11,10},{13,12},{... | collective-permute-start | bytes 196616 | tf_op jit(solution)/shard_map/ppermute | solution.py:20
  274.3 3.6 %collective-permute-done.31 = f32[1,128,128]{2,1,0:T(8,128)S(1)} collective-permute-done((f32[1,128,128]{2,1,0:T(8,128)S(1)}, f32[1,128,128]{2,1,0:T(8,128)S(1)}, u32[]{:S(2)}, u32[]{:S(2)}) %collective-permute-start.31) | collective-permute-done | bytes 65568 | tf_op jit(solution)/shard_map/ppermute | solution.py:17
  282.4 3.2 %collective-permute-done.33 = f32[1,128,128]{2,1,0:T(8,128)S(1)} collective-permute-done((f32[1,128,128]{2,1,0:T(8,128)S(1)}, f32[1,128,128]{2,1,0:T(8,128)S(1)}, u32[]{:S(2)}, u32[]{:S(2)}) %collective-permute-start.33) | collective-permute-done | bytes 65568 | tf_op jit(solution)/shard_map/ppermute | solution.py:17
  (157 shorter events, 97.5 us)
Async XLA Ops:
  6.5 78.6 %all-gather.9.cloned.1.call-start = ((), (), s32[]{:S(2)}) async-start(), calls=%async_computation | async-start | bytes 1179648 | tf_op jit(solution)/shard_map/all_gather | solution.py:33
  6.5 7.3 %collective-permute-start = (f32[2,128,128]{2,1,0:T(8,128)}, f32[2,128,128]{2,1,0:T(8,128)S(1)}, u32[]{:S(2)}, u32[]{:S(2)}) collective-permute-start(f32[2,128,128]{2,1,0:T(8,128)} %bitcast.276), channel_id=1, source_target_pairs={{0,4},{4,8},{8,12},{12,16},{16,20},{20,24},{24,28},{1,5},{5,9},{9,... | collective-permute-start | bytes 393224 | tf_op jit(solution)/shard_map/ppermute | solution.py:28
  14.9 6.6 %collective-permute-start.1 = (f32[5,1,128,128]{3,2,1,0:T(8,128)S(1)}, f32[5,1,128,128]{3,2,1,0:T(8,128)S(1)}, u32[]{:S(2)}, u32[]{:S(2)}) collective-permute-start(f32[5,1,128,128]{3,2,1,0:T(8,128)S(1)} %get-tuple-element.165), channel_id=1, source_target_pairs={{1,0},{2,1},{3,2},{5,4},{6,5},{7,6},{9,8},{10,9},{11,10},{13,12},{... | collective-permute-start | bytes 983048 | tf_op jit(solution)/shard_map/ppermute | solution.py:20
  17.0 8.4 %collective-permute-start.2 = (f32[5,1,128,128]{3,2,1,0:T(8,128)S(1)}, f32[5,1,128,128]{3,2,1,0:T(8,128)S(1)}, u32[]{:S(2)}, u32[]{:S(2)}) collective-permute-start(f32[5,1,128,128]{3,2,1,0:T(8,128)S(1)} %get-tuple-element.166), channel_id=1, source_target_pairs={{0,1},{1,2},{2,3},{4,5},{5,6},{6,7},{8,9},{9,10},{10,11},{12,13},{... | collective-permute-start | bytes 983048 | tf_op jit(solution)/shard_map/ppermute | solution.py:17
  25.9 5.2 %collective-permute-start.3 = (f32[1,128,128]{2,1,0:T(8,128)S(1)}, f32[1,128,128]{2,1,0:T(8,128)S(1)}, u32[]{:S(2)}, u32[]{:S(2)}) collective-permute-start(f32[1,128,128]{2,1,0:T(8,128)S(1)} %get-tuple-element.193), channel_id=1, source_target_pairs={{1,0},{2,1},{3,2},{5,4},{6,5},{7,6},{9,8},{10,9},{11,10},{13,12},{... | collective-permute-start | bytes 196616 | tf_op jit(solution)/shard_map/ppermute | solution.py:20
  27.8 5.6 %collective-permute-start.4 = (f32[1,128,128]{2,1,0:T(8,128)S(1)}, f32[1,128,128]{2,1,0:T(8,128)S(1)}, u32[]{:S(2)}, u32[]{:S(2)}) collective-permute-start(f32[1,128,128]{2,1,0:T(8,128)S(1)} %get-tuple-element.194), channel_id=1, source_target_pairs={{0,1},{1,2},{2,3},{4,5},{5,6},{6,7},{8,9},{9,10},{10,11},{12,13},{... | collective-permute-start | bytes 196616 | tf_op jit(solution)/shard_map/ppermute | solution.py:17
  31.0 83.9 %all-gather.11.cloned.1.call-start = ((), (), s32[]{:S(2)}) async-start(), calls=%async_computation.1 | async-start | bytes 1179648 | tf_op jit(solution)/shard_map/all_gather | solution.py:33
  33.6 4.4 %collective-permute-start.5 = (f32[1,128,128]{2,1,0:T(8,128)S(1)}, f32[1,128,128]{2,1,0:T(8,128)S(1)}, u32[]{:S(2)}, u32[]{:S(2)}) collective-permute-start(f32[1,128,128]{2,1,0:T(8,128)S(1)} %get-tuple-element.191), channel_id=1, source_target_pairs={{1,0},{2,1},{3,2},{5,4},{6,5},{7,6},{9,8},{10,9},{11,10},{13,12},{... | collective-permute-start | bytes 196616 | tf_op jit(solution)/shard_map/ppermute | solution.py:20
  35.5 5.6 %collective-permute-start.6 = (f32[1,128,128]{2,1,0:T(8,128)S(1)}, f32[1,128,128]{2,1,0:T(8,128)S(1)}, u32[]{:S(2)}, u32[]{:S(2)}) collective-permute-start(f32[1,128,128]{2,1,0:T(8,128)S(1)} %get-tuple-element.192), channel_id=1, source_target_pairs={{0,1},{1,2},{2,3},{4,5},{5,6},{6,7},{8,9},{9,10},{10,11},{12,13},{... | collective-permute-start | bytes 196616 | tf_op jit(solution)/shard_map/ppermute | solution.py:17
  41.3 4.4 %collective-permute-start.7 = (f32[1,128,128]{2,1,0:T(8,128)S(1)}, f32[1,128,128]{2,1,0:T(8,128)S(1)}, u32[]{:S(2)}, u32[]{:S(2)}) collective-permute-start(f32[1,128,128]{2,1,0:T(8,128)S(1)} %get-tuple-element.189), channel_id=1, source_target_pairs={{1,0},{2,1},{3,2},{5,4},{6,5},{7,6},{9,8},{10,9},{11,10},{13,12},{... | collective-permute-start | bytes 196616 | tf_op jit(solution)/shard_map/ppermute | solution.py:20
  43.2 5.6 %collective-permute-start.8 = (f32[1,128,128]{2,1,0:T(8,128)S(1)}, f32[1,128,128]{2,1,0:T(8,128)S(1)}, u32[]{:S(2)}, u32[]{:S(2)}) collective-permute-start(f32[1,128,128]{2,1,0:T(8,128)S(1)} %get-tuple-element.190), channel_id=1, source_target_pairs={{0,1},{1,2},{2,3},{4,5},{5,6},{6,7},{8,9},{9,10},{10,11},{12,13},{... | collective-permute-start | bytes 196616 | tf_op jit(solution)/shard_map/ppermute | solution.py:17
  49.0 5.6 %collective-permute-start.10 = (f32[1,128,128]{2,1,0:T(8,128)S(1)}, f32[1,128,128]{2,1,0:T(8,128)S(1)}, u32[]{:S(2)}, u32[]{:S(2)}) collective-permute-start(f32[1,128,128]{2,1,0:T(8,128)S(1)} %get-tuple-element.188), channel_id=1, source_target_pairs={{0,1},{1,2},{2,3},{4,5},{5,6},{6,7},{8,9},{9,10},{10,11},{12,13},{... | collective-permute-start | bytes 196616 | tf_op jit(solution)/shard_map/ppermute | solution.py:17
  50.9 5.5 %collective-permute-start.9 = (f32[1,128,128]{2,1,0:T(8,128)S(1)}, f32[1,128,128]{2,1,0:T(8,128)S(1)}, u32[]{:S(2)}, u32[]{:S(2)}) collective-permute-start(f32[1,128,128]{2,1,0:T(8,128)S(1)} %get-tuple-element.187), channel_id=1, source_target_pairs={{1,0},{2,1},{3,2},{5,4},{6,5},{7,6},{9,8},{10,9},{11,10},{13,12},{... | collective-permute-start | bytes 196616 | tf_op jit(solution)/shard_map/ppermute | solution.py:20
  56.6 5.7 %collective-permute-start.11 = (f32[1,128,128]{2,1,0:T(8,128)S(1)}, f32[1,128,128]{2,1,0:T(8,128)S(1)}, u32[]{:S(2)}, u32[]{:S(2)}) collective-permute-start(f32[1,128,128]{2,1,0:T(8,128)S(1)} %get-tuple-element.185), channel_id=1, source_target_pairs={{1,0},{2,1},{3,2},{5,4},{6,5},{7,6},{9,8},{10,9},{11,10},{13,12},{... | collective-permute-start | bytes 196616 | tf_op jit(solution)/shard_map/ppermute | solution.py:20
  60.3 5.6 %collective-permute-start.12 = (f32[1,128,128]{2,1,0:T(8,128)S(1)}, f32[1,128,128]{2,1,0:T(8,128)S(1)}, u32[]{:S(2)}, u32[]{:S(2)}) collective-permute-start(f32[1,128,128]{2,1,0:T(8,128)S(1)} %get-tuple-element.186), channel_id=1, source_target_pairs={{0,1},{1,2},{2,3},{4,5},{5,6},{6,7},{8,9},{9,10},{10,11},{12,13},{... | collective-permute-start | bytes 196616 | tf_op jit(solution)/shard_map/ppermute | solution.py:17
  75.5 177.3 %all-gather.13.cloned.1.call-start = ((), (), s32[]{:S(2)}) async-start(), calls=%async_computation.2 | async-start | bytes 1179648 | tf_op jit(solution)/shard_map/all_gather | solution.py:33
  131.4 5.0 %collective-permute-start.13 = (f32[1,128,128]{2,1,0:T(8,128)S(1)}, f32[1,128,128]{2,1,0:T(8,128)S(1)}, u32[]{:S(2)}, u32[]{:S(2)}) collective-permute-start(f32[1,128,128]{2,1,0:T(8,128)S(1)} %get-tuple-element.183), channel_id=1, source_target_pairs={{1,0},{2,1},{3,2},{5,4},{6,5},{7,6},{9,8},{10,9},{11,10},{13,12},{... | collective-permute-start | bytes 196616 | tf_op jit(solution)/shard_map/ppermute | solution.py:20
  134.5 5.6 %collective-permute-start.14 = (f32[1,128,128]{2,1,0:T(8,128)S(1)}, f32[1,128,128]{2,1,0:T(8,128)S(1)}, u32[]{:S(2)}, u32[]{:S(2)}) collective-permute-start(f32[1,128,128]{2,1,0:T(8,128)S(1)} %get-tuple-element.184), channel_id=1, source_target_pairs={{0,1},{1,2},{2,3},{4,5},{5,6},{6,7},{8,9},{9,10},{10,11},{12,13},{... | collective-permute-start | bytes 196616 | tf_op jit(solution)/shard_map/ppermute | solution.py:17
  142.1 5.6 %collective-permute-start.16 = (f32[1,128,128]{2,1,0:T(8,128)S(1)}, f32[1,128,128]{2,1,0:T(8,128)S(1)}, u32[]{:S(2)}, u32[]{:S(2)}) collective-permute-start(f32[1,128,128]{2,1,0:T(8,128)S(1)} %get-tuple-element.182), channel_id=1, source_target_pairs={{0,1},{1,2},{2,3},{4,5},{5,6},{6,7},{8,9},{9,10},{10,11},{12,13},{... | collective-permute-start | bytes 196616 | tf_op jit(solution)/shard_map/ppermute | solution.py:17
  148.1 6.9 %collective-permute-start.17 = (f32[2,128,128]{2,1,0:T(8,128)S(1)}, f32[2,128,128]{2,1,0:T(8,128)S(1)}, u32[]{:S(2)}, u32[]{:S(2)}) collective-permute-start(f32[2,128,128]{2,1,0:T(8,128)S(1)} %get-tuple-element.142), channel_id=1, source_target_pairs={{0,4},{4,8},{8,12},{12,16},{16,20},{20,24},{24,28},{1,5},{5,9},{9,... | collective-permute-start | bytes 393224 | tf_op jit(solution)/shard_map/ppermute | solution.py:28
  155.0 6.5 %collective-permute-start.18 = (f32[5,1,128,128]{3,2,1,0:T(8,128)S(1)}, f32[5,1,128,128]{3,2,1,0:T(8,128)S(1)}, u32[]{:S(2)}, u32[]{:S(2)}) collective-permute-start(f32[5,1,128,128]{3,2,1,0:T(8,128)S(1)} %get-tuple-element.163), channel_id=1, source_target_pairs={{1,0},{2,1},{3,2},{5,4},{6,5},{7,6},{9,8},{10,9},{11,10},{13,12},{... | collective-permute-start | bytes 983048 | tf_op jit(solution)/shard_map/ppermute | solution.py:20
  156.9 8.4 %collective-permute-start.19 = (f32[5,1,128,128]{3,2,1,0:T(8,128)S(1)}, f32[5,1,128,128]{3,2,1,0:T(8,128)S(1)}, u32[]{:S(2)}, u32[]{:S(2)}) collective-permute-start(f32[5,1,128,128]{3,2,1,0:T(8,128)S(1)} %get-tuple-element.164), channel_id=1, source_target_pairs={{0,1},{1,2},{2,3},{4,5},{5,6},{6,7},{8,9},{9,10},{10,11},{12,13},{... | collective-permute-start | bytes 983048 | tf_op jit(solution)/shard_map/ppermute | solution.py:17
  167.8 5.6 %collective-permute-start.21 = (f32[1,128,128]{2,1,0:T(8,128)S(1)}, f32[1,128,128]{2,1,0:T(8,128)S(1)}, u32[]{:S(2)}, u32[]{:S(2)}) collective-permute-start(f32[1,128,128]{2,1,0:T(8,128)S(1)} %get-tuple-element.180), channel_id=1, source_target_pairs={{0,1},{1,2},{2,3},{4,5},{5,6},{6,7},{8,9},{9,10},{10,11},{12,13},{... | collective-permute-start | bytes 196616 | tf_op jit(solution)/shard_map/ppermute | solution.py:17
  173.5 4.5 %collective-permute-start.22 = (f32[1,128,128]{2,1,0:T(8,128)S(1)}, f32[1,128,128]{2,1,0:T(8,128)S(1)}, u32[]{:S(2)}, u32[]{:S(2)}) collective-permute-start(f32[1,128,128]{2,1,0:T(8,128)S(1)} %get-tuple-element.177), channel_id=1, source_target_pairs={{1,0},{2,1},{3,2},{5,4},{6,5},{7,6},{9,8},{10,9},{11,10},{13,12},{... | collective-permute-start | bytes 196616 | tf_op jit(solution)/shard_map/ppermute | solution.py:20
  175.5 5.6 %collective-permute-start.23 = (f32[1,128,128]{2,1,0:T(8,128)S(1)}, f32[1,128,128]{2,1,0:T(8,128)S(1)}, u32[]{:S(2)}, u32[]{:S(2)}) collective-permute-start(f32[1,128,128]{2,1,0:T(8,128)S(1)} %get-tuple-element.178), channel_id=1, source_target_pairs={{0,1},{1,2},{2,3},{4,5},{5,6},{6,7},{8,9},{9,10},{10,11},{12,13},{... | collective-permute-start | bytes 196616 | tf_op jit(solution)/shard_map/ppermute | solution.py:17
  183.1 5.6 %collective-permute-start.25 = (f32[1,128,128]{2,1,0:T(8,128)S(1)}, f32[1,128,128]{2,1,0:T(8,128)S(1)}, u32[]{:S(2)}, u32[]{:S(2)}) collective-permute-start(f32[1,128,128]{2,1,0:T(8,128)S(1)} %get-tuple-element.176), channel_id=1, source_target_pairs={{0,1},{1,2},{2,3},{4,5},{5,6},{6,7},{8,9},{9,10},{10,11},{12,13},{... | collective-permute-start | bytes 196616 | tf_op jit(solution)/shard_map/ppermute | solution.py:17
  190.8 5.6 %collective-permute-start.27 = (f32[1,128,128]{2,1,0:T(8,128)S(1)}, f32[1,128,128]{2,1,0:T(8,128)S(1)}, u32[]{:S(2)}, u32[]{:S(2)}) collective-permute-start(f32[1,128,128]{2,1,0:T(8,128)S(1)} %get-tuple-element.174), channel_id=1, source_target_pairs={{0,1},{1,2},{2,3},{4,5},{5,6},{6,7},{8,9},{9,10},{10,11},{12,13},{... | collective-permute-start | bytes 196616 | tf_op jit(solution)/shard_map/ppermute | solution.py:17
  196.6 4.4 %collective-permute-start.28 = (f32[1,128,128]{2,1,0:T(8,128)S(1)}, f32[1,128,128]{2,1,0:T(8,128)S(1)}, u32[]{:S(2)}, u32[]{:S(2)}) collective-permute-start(f32[1,128,128]{2,1,0:T(8,128)S(1)} %get-tuple-element.171), channel_id=1, source_target_pairs={{1,0},{2,1},{3,2},{5,4},{6,5},{7,6},{9,8},{10,9},{11,10},{13,12},{... | collective-permute-start | bytes 196616 | tf_op jit(solution)/shard_map/ppermute | solution.py:20
  198.5 5.6 %collective-permute-start.29 = (f32[1,128,128]{2,1,0:T(8,128)S(1)}, f32[1,128,128]{2,1,0:T(8,128)S(1)}, u32[]{:S(2)}, u32[]{:S(2)}) collective-permute-start(f32[1,128,128]{2,1,0:T(8,128)S(1)} %get-tuple-element.172), channel_id=1, source_target_pairs={{0,1},{1,2},{2,3},{4,5},{5,6},{6,7},{8,9},{9,10},{10,11},{12,13},{... | collective-permute-start | bytes 196616 | tf_op jit(solution)/shard_map/ppermute | solution.py:17
  269.3 5.0 %collective-permute-start.30 = (f32[1,128,128]{2,1,0:T(8,128)S(1)}, f32[1,128,128]{2,1,0:T(8,128)S(1)}, u32[]{:S(2)}, u32[]{:S(2)}) collective-permute-start(f32[1,128,128]{2,1,0:T(8,128)S(1)} %get-tuple-element.169), channel_id=1, source_target_pairs={{1,0},{2,1},{3,2},{5,4},{6,5},{7,6},{9,8},{10,9},{11,10},{13,12},{... | collective-permute-start | bytes 196616 | tf_op jit(solution)/shard_map/ppermute | solution.py:20
  272.3 5.6 %collective-permute-start.31 = (f32[1,128,128]{2,1,0:T(8,128)S(1)}, f32[1,128,128]{2,1,0:T(8,128)S(1)}, u32[]{:S(2)}, u32[]{:S(2)}) collective-permute-start(f32[1,128,128]{2,1,0:T(8,128)S(1)} %get-tuple-element.170), channel_id=1, source_target_pairs={{0,1},{1,2},{2,3},{4,5},{5,6},{6,7},{8,9},{9,10},{10,11},{12,13},{... | collective-permute-start | bytes 196616 | tf_op jit(solution)/shard_map/ppermute | solution.py:17
  280.0 5.6 %collective-permute-start.33 = (f32[1,128,128]{2,1,0:T(8,128)S(1)}, f32[1,128,128]{2,1,0:T(8,128)S(1)}, u32[]{:S(2)}, u32[]{:S(2)}) collective-permute-start(f32[1,128,128]{2,1,0:T(8,128)S(1)} %get-tuple-element.168), channel_id=1, source_target_pairs={{0,1},{1,2},{2,3},{4,5},{5,6},{6,7},{8,9},{9,10},{10,11},{12,13},{... | collective-permute-start | bytes 196616 | tf_op jit(solution)/shard_map/ppermute | solution.py:17
  (8 other events, 34.9 us)
Sparse Core Ops, SparseCore 0:
  31.2 38.9 all-gather.8
  75.6 39.3 all-gather.10
  213.8 38.9 all-gather.12
where the time goes:
time: 295 us; the launch traced here: 293 us
  waiting for transfers between devices  135 us (46%)
  starting transfers between devices  76.1 us (26%)
  blocking collectives  33.3 us (11%)
  other arithmetic  18.9 us (6%)
  between operations  14.8 us (5%)
  matrix products  9.32 us (3%)
  local copies, waits for them, and re-layouts  5.59 us (2%)
    all_gather x3, waiting for transfers between devices, prefix(): gathered = jax.tree.map(lambda a: lax.all_gather(a, axis), part)  68.9 us
    ppermute x16, waiting for transfers between devices, with_halo(): lax.ppermute(lax.slice_in_dim(block, block.shape[dim] - width, None, axis...  49 us
    ppermute x16, starting transfers between devices, with_halo(): lax.ppermute(lax.slice_in_dim(block, block.shape[dim] - width, None, axis...  36.8 us
    ppermute x16, starting transfers between devices, with_halo(): lax.ppermute(lax.slice_in_dim(block, 0, width, axis=dim), axis, backward)  36.6 us
    all_gather x3, blocking collectives, forward(): shard_rows = lax.all_gather(flat, 'space', axis=0, tiled=True)  20.3 us
    add x14, other arithmetic, compose(): return (earlier[0] * later[0], later[0] * earlier[1] + later[1])  14.7 us
    all_gather x2, blocking collectives, body(): lax.all_gather(inverse_flat, 'space', axis=0, tiled=True)  13 us
    ppermute x2, waiting for transfers between devices, shifted(): lax.ppermute(value, axis, [(source, source + steps) for source in range(f...  10.9 us
  transfers between devices with their start and end apart: 37, of which 22 were waited for; matrix products, arithmetic and copies ran while one was open for 2% of the time, Pallas kernels for 0%

commit v1 on v0

v1 whole, which is shorter than its diff:
```python
import functools
import math

import jax
import jax.numpy as jnp
import numpy as np
from jax import lax
from jax.experimental import pallas as pl
from jax.experimental.pallas import tpu as pltpu
from jax.sharding import PartitionSpec as P

MESH = pl.DeviceIdType.MESH
CHUNKS = 2


def node_tables():
    radical = math.sqrt(3.0 / 7.0)
    node_times = [0.0, (1.0 - radical) / 2.0, 0.5, (1.0 + radical) / 2.0, 1.0]
    integrals = np.zeros((4, 5))
    for column in range(5):
        coeffs = [1.0]
        for other_index in range(5):
            if other_index == column:
                continue
            other_time = node_times[other_index]
            scaling = node_times[column] - other_time
            grown = [0.0] * (len(coeffs) + 1)
            for exponent in range(len(coeffs)):
                grown[exponent + 1] += coeffs[exponent] / scaling
                grown[exponent] -= coeffs[exponent] * other_time / scaling
            coeffs = grown
        for section in range(4):
            integrals[section, column] = sum(
                (
                    coeffs[exponent]
                    * (
                        node_times[section + 1] ** (exponent + 1)
                        - node_times[section] ** (exponent + 1)
                    )
                    / (exponent + 1)
                    for exponent in range(len(coeffs))
                )
            )
    coarse = [0.0, 0.5, 1.0]
    interp = np.zeros((5, 3))
    for column in range(3):
        for section in range(5):
            weight = 1.0
            for other_index in range(3):
                if other_index != column:
                    weight = (
                        weight
                        * (node_times[section] - coarse[other_index])
                        / (coarse[column] - coarse[other_index])
                    )
            interp[section, column] = weight
    return (np.array(node_times), integrals, interp)


def sine(length):
    k = np.arange(1, length + 1)
    phase = np.outer(k, k) % (2 * (length + 1))
    return math.sqrt(2.0 / (length + 1)) * np.sin(math.pi / (length + 1) * phase)


def eigen(length):
    return 2.0 - 2.0 * np.cos(math.pi / (length + 1) * np.arange(1, length + 1))


def split_pair(value):
    high = value.astype(jnp.bfloat16)
    return high, (value - high.astype(jnp.float32)).astype(jnp.bfloat16)


def dot(a, b):
    return jnp.dot(a, b, preferred_element_type=jnp.float32)


def precise(a, b):
    return dot(a[0], b[0]) + (dot(a[1], b[0]) + dot(a[0], b[1]))


def lateral(field, x_pair, y_pair):
    depth, width_x, width_y = field.shape
    mixed = precise(split_pair(field.reshape(depth * width_x, width_y)), y_pair)
    return [
        precise(x_pair, split_pair(mixed[z * width_x : (z + 1) * width_x])) for z in range(depth)
    ]


def z_sine(planes):
    count = len(planes)
    table = sine(count)
    half = (count + 1) // 2
    pairs = [
        (planes[z] + planes[count - 1 - z], planes[z] - planes[count - 1 - z])
        if z != count - 1 - z
        else (planes[z], None)
        for z in range(half)
    ]
    out = []
    for k in range(count):
        terms = [
            float(table[k, z]) * pairs[z][k % 2] for z in range(half) if pairs[z][k % 2] is not None
        ]
        total = terms[0]
        for term in terms[1:]:
            total = total + term
        out.append(total)
    return out


def weighted(weights, items):
    total = None
    for weight, item in zip(weights, items):
        weight = float(weight)
        if weight == 0.0 or item is None:
            continue
        term = item if weight == 1.0 else weight * item
        total = term if total is None else total + term
    return total


def sweep(rate, nodes, sources):
    times, integrals, _ = TABLES
    swept = [nodes[0]]
    for m in range(4):
        spacing = float(times[m + 1] - times[m])
        inner = weighted(integrals[m], nodes)
        if m > 0:
            inner = inner + spacing * (swept[m] - nodes[m])
        step = rate * inner
        if swept[m] is not None:
            step = step + swept[m]
        if sources is not None:
            step = step + sources[m]
        swept.append(step)
    first = list(integrals[0] + integrals[1])
    second = list(integrals[2] + integrals[3])
    first[0] -= 0.5
    second[2] -= 0.5
    left = rate * weighted(first, swept)
    right = rate * weighted(second, swept)
    if sources is not None:
        left = left + (sources[0] + sources[1])
        right = right + (sources[2] + sources[3])
    return swept, left, right


def corrected(swept, left, right, middle):
    interp = TABLES[2]
    ending = middle * left + right
    deltas = [None if swept[0] is None else -swept[0], left - swept[2], ending - swept[4]]
    return [
        None,
        swept[1] + weighted(interp[1], deltas),
        left,
        swept[3] + weighted(interp[3], deltas),
        ending,
    ]


def start_gains(middle):
    interp = TABLES[2]
    square = middle * middle
    return [
        None,
        float(interp[1, 0]) + float(interp[1, 1]) * middle + float(interp[1, 2]) * square,
        middle,
        float(interp[3, 0]) + float(interp[3, 1]) * middle + float(interp[3, 2]) * square,
        square,
    ]


def gains_of(rate):
    middle = 1.0 + 0.5 * rate
    gains = start_gains(middle)
    nodes = [jnp.ones_like(middle)] + gains[1:]
    swept, left, right = sweep(rate, nodes, None)
    return gains, corrected(swept, left, right, middle)


TABLES = node_tables()


def kernel(
    dims,
    step_ref, initial_hbm, guess_hbm, forcing_hbm, x_ref, y_ref, lateral_ref,
    out_hbm,
    initial, guess, forcing, result,
    in_send, in_recv, ghat, hhat, ell, own_step, steps,
    gain_c, gain_d, part_b, z_send, z_recv, own_gain, own_cross, r_send, r_recv,
    o_send, o_recv,
    load_sem, store_sem, in_ss, in_rs, h_ss, h_rs, s_ss, s_rs, z_ss, z_rs, r_ss, r_rs, o_ss, o_rs,
):
    spaces, slices, chunks, depth, length_z, rows, width_y, owners, block = dims
    me = lax.axis_index("space")
    place = lax.axis_index("tm")
    _, integrals, _ = TABLES
    width_x = spaces * chunks * rows

    load_guess = pltpu.make_async_copy(guess_hbm.at[0], guess, load_sem.at[0])
    load_forcing = pltpu.make_async_copy(forcing_hbm.at[0], forcing, load_sem.at[1])
    load_initial = pltpu.make_async_copy(initial_hbm, initial, load_sem.at[2])
    load_guess.start()
    load_forcing.start()
    load_initial.start()

    barrier = pltpu.get_barrier_semaphore()
    for i in range(1, spaces):
        pl.semaphore_signal(
            barrier, inc=1, device_id={"space": lax.rem(me + i, spaces)}, device_id_type=MESH
        )

    def greet(i, carry):
        pl.semaphore_signal(
            barrier, inc=1, device_id={"tm": lax.rem(place + i, slices)}, device_id_type=MESH
        )
        return carry

    lax.fori_loop(1, slices, greet, 0)

    step = step_ref[0]
    x_pair = (x_ref[0], x_ref[1])
    y_pair = (y_ref[0], y_ref[1])
    own_step[...] = jnp.full(own_step.shape, step, jnp.float32)
    steps[place] = jnp.full(own_step.shape, step, jnp.float32)

    def put(field, slot):
        planes = lateral(field, x_pair, y_pair)
        for target in range(spaces):
            for c in range(chunks):
                low = (target * chunks + c) * rows
                for z in range(depth):
                    in_send[c, target, slot, z] = planes[z][low : low + rows]

    def keep(c, low, high):
        in_recv[c, me, low:high] = in_send[c, me, low:high]

    groups = ((0, 1), (1, 5), (5, 6))

    def in_copy(c, group, peer, source):
        low, high = groups[group]
        return pltpu.make_async_remote_copy(
            src_ref=in_send.at[c, peer, low:high],
            dst_ref=in_recv.at[c, source, low:high],
            send_sem=in_ss.at[c, group, peer],
            recv_sem=in_rs.at[c, group, source],
            device_id={"space": peer},
            device_id_type=MESH,
        )

    def in_start(c, group):
        for i in range(1, spaces):
            in_copy(c, group, lax.rem(me + i, spaces), me).start()

    def in_wait(c, group):
        for i in range(1, spaces):
            peer = lax.rem(me + i, spaces)
            in_copy(c, group, peer, peer).wait_recv()

    load_guess.wait()
    put(guess[...], 0)
    pl.semaphore_wait(barrier, spaces - 1 + slices - 1)
    for c in range(chunks):
        in_start(c, 0)

    def step_copy(peer, source):
        return pltpu.make_async_remote_copy(
            src_ref=own_step,
            dst_ref=steps.at[source],
            send_sem=s_ss.at[peer],
            recv_sem=s_rs.at[source],
            device_id={"tm": peer},
            device_id_type=MESH,
        )

    def peers(action):
        def one(i, carry):
            action(lax.rem(place + i, slices))
            return carry

        lax.fori_loop(1, slices, one, 0)

    peers(lambda peer: step_copy(peer, place).start())

    for c in range(chunks):
        keep(c, 0, 1)
    load_forcing.wait()
    for m in range(4):
        put(step * weighted(integrals[m], [forcing[j] for j in range(5)]), m + 1)
    for c in range(chunks):
        in_start(c, 1)
        keep(c, 1, 5)
    load_initial.wait()

    @pl.when(place == 0)
    def _():
        put(initial[...], 5)
        for c in range(chunks):
            in_start(c, 2)
            keep(c, 5, 6)

    z_eigen = eigen(length_z)
    for c in range(chunks):
        low = pl.multiple_of((me * chunks + c) * rows, 8)
        base = lateral_ref[pl.ds(low, rows), :]
        for k in range(length_z):
            ell[c, k * rows : (k + 1) * rows] = -(base + float(z_eigen[k]))

    def table(i, carry):
        for c in range(chunks):
            at = pl.ds(pl.multiple_of(i * rows, 8), rows)
            gains, crossed = gains_of(step * ell[c, at])
            for m in range(1, 5):
                gain_c[c, m - 1, at] = gains[m]
                gain_d[c, m - 1, at] = crossed[m]
        return carry

    lax.fori_loop(0, length_z, table, 0)

    def planes_of(c, slot):
        return [in_recv[c, z // depth, slot, z % depth] for z in range(length_z)]

    def h_copy(c, peer):
        return pltpu.make_async_remote_copy(
            src_ref=ghat.at[c],
            dst_ref=hhat.at[c],
            send_sem=h_ss.at[c],
            recv_sem=h_rs.at[c],
            device_id={"tm": peer},
            device_id_type=MESH,
        )

    after = lax.rem(place + 1, slices)
    for c in range(chunks):
        in_wait(c, 0)
        for k, plane in enumerate(z_sine(planes_of(c, 0))):
            ghat[c, k * rows : (k + 1) * rows] = plane

        @pl.when(place < slices - 1)
        def _():
            h_copy(c, after).start()

    peers(lambda peer: step_copy(peer, peer).wait_recv())

    @pl.when(place < owners)
    def _():
        def one(p, carry):
            for c in range(chunks):
                at = pl.ds(pl.multiple_of(place * block, 8), block)
                gains, crossed = gains_of(steps[p][0:1] * ell[c, at])
                own_gain[c, p] = gains[4]
                own_cross[c, p] = crossed[4]
            return carry

        lax.fori_loop(0, slices, one, 0)

    def z_copy(c, owner, source):
        return pltpu.make_async_remote_copy(
            src_ref=z_send.at[c, owner],
            dst_ref=z_recv.at[c, source],
            send_sem=z_ss.at[c, owner],
            recv_sem=z_rs.at[c, source],
            device_id={"tm": owner},
            device_id_type=MESH,
        )

    def to_owner(owner, action):
        if owners == slices:
            action()
        else:
            pl.when(owner < owners)(action)

    first = jnp.where(place == 0, 1.0, 0.0).astype(jnp.float32)
    for c in range(chunks):
        in_wait(c, 1)
        fhat = [z_sine(planes_of(c, m + 1)) for m in range(4)]
        for m in range(4):
            for k in range(length_z):
                part_b[c, m, k * rows : (k + 1) * rows] = fhat[m][k]

        @pl.when(place == 0)
        def _():
            in_wait(c, 2)
            for k, plane in enumerate(z_sine(planes_of(c, 5))):
                hhat[c, k * rows : (k + 1) * rows] = plane

        @pl.when(place > 0)
        def _():
            h_copy(c, after).wait_recv()

        def solve(i, carry):
            at = pl.ds(pl.multiple_of(i * block, 8), block)
            rate = step * ell[c, at]
            middle = 1.0 + 0.5 * rate
            guess_hat, start = ghat[c, at], hhat[c, at]
            sources = [part_b[c, m, at] for m in range(4)]
            one = sweep(rate, [start] + [guess_hat] * 4, sources)
            nodes = corrected(*one, middle)
            rest = corrected(*sweep(rate, nodes, sources), middle)
            for m in range(1, 5):
                part_b[c, m - 1, at] = rest[m]
            seen = first * start
            gain, cross = gain_c[c, 3, at], gain_d[c, 3, at]
            z_send[c, i, 0] = nodes[4] + gain * seen
            z_send[c, i, 1] = rest[4] + (gain + cross) * seen
            return carry

        lax.fori_loop(0, owners, solve, 0)
        peers(lambda peer: to_owner(peer, lambda: z_copy(c, peer, place).start()))

        @pl.when(place < owners)
        def _():
            z_recv[c, place] = z_send[c, place]

    def r_copy(c, target, owner):
        return pltpu.make_async_remote_copy(
            src_ref=r_send.at[c, target],
            dst_ref=r_recv.at[c, owner],
            send_sem=r_ss.at[c, target],
            recv_sem=r_rs.at[c, owner],
            device_id={"tm": target},
            device_id_type=MESH,
        )

    for c in range(chunks):
        @pl.when(place < owners)
        def _():
            peers(lambda peer: z_copy(c, peer, peer).wait_recv())

            def scan(p, state):
                lower, upper = state
                r_send[c, p, 0] = lower
                r_send[c, p, 1] = upper
                gain = own_gain[c, p]
                return (
                    gain * lower + z_recv[c, p, 0],
                    gain * upper + own_cross[c, p] * lower + z_recv[c, p, 1],
                )

            zero = jnp.zeros((block, width_y), jnp.float32)
            lax.fori_loop(0, slices, scan, (zero, zero))
            peers(lambda peer: r_copy(c, peer, place).start())
            r_recv[c, place] = r_send[c, place]

    def o_copy(c, m, peer, source):
        return pltpu.make_async_remote_copy(
            src_ref=o_send.at[c, peer, m],
            dst_ref=o_recv.at[c, source, m],
            send_sem=o_ss.at[c, m, peer],
            recv_sem=o_rs.at[c, m, source],
            device_id={"space": peer},
            device_id_type=MESH,
        )

    for c in range(chunks):
        peers(lambda peer: to_owner(peer, lambda: r_copy(c, peer, peer).wait_recv()))
        own = hhat[c].reshape(owners, block, width_y)
        lower = jnp.where(place == 0, own, r_recv[c, :, 0]).reshape(length_z * rows, width_y)
        upper = jnp.where(place == 0, own, r_recv[c, :, 1]).reshape(length_z * rows, width_y)
        for m in range(5):
            if m == 0:
                value = upper
            else:
                value = (
                    gain_c[c, m - 1] * upper + gain_d[c, m - 1] * lower + part_b[c, m - 1]
                )
            planes = z_sine([value[k * rows : (k + 1) * rows] for k in range(length_z)])
            for z in range(length_z):
                o_send[c, z // depth, m, z % depth] = planes[z]
            for i in range(1, spaces):
                o_copy(c, m, lax.rem(me + i, spaces), me).start()
            o_recv[c, me, m] = o_send[c, me, m]

    def store(m):
        return pltpu.make_async_copy(result.at[m], out_hbm.at[0, m], store_sem.at[m])

    for m in range(5):
        for c in range(chunks):
            for i in range(1, spaces):
                peer = lax.rem(me + i, spaces)
                o_copy(c, m, peer, peer).wait_recv()
        field = jnp.stack(
            [
                jnp.concatenate(
                    [o_recv[c, s, m, z] for s in range(spaces) for c in range(chunks)], axis=0
                )
                for z in range(depth)
            ]
        )
        planes = lateral(field, x_pair, y_pair)
        for z in range(depth):
            result[m, z] = planes[z]
        store(m).start()

    for c in range(chunks):
        for i in range(1, spaces):
            peer = lax.rem(me + i, spaces)
            in_copy(c, 0, peer, me).wait_send()
            in_copy(c, 1, peer, me).wait_send()
            for m in range(5):
                o_copy(c, m, peer, me).wait_send()

        @pl.when(place == 0)
        def _():
            for i in range(1, spaces):
                in_copy(c, 2, lax.rem(me + i, spaces), me).wait_send()

        @pl.when(place < slices - 1)
        def _():
            h_copy(c, after).wait_send()

        peers(lambda peer: to_owner(peer, lambda: z_copy(c, peer, place).wait_send()))

        @pl.when(place < owners)
        def _():
            peers(lambda peer: r_copy(c, peer, place).wait_send())

    peers(lambda peer: step_copy(peer, place).wait_send())
    for m in range(5):
        store(m).wait()


def body(initial, start_guess, forcing, step_size):
    depth, width_x, width_y = initial.shape
    spaces, slices = lax.axis_size("space"), lax.axis_size("tm")
    length_z = depth * spaces
    chunks = CHUNKS
    rows = width_x // spaces // chunks
    owners = min(slices, length_z * rows // 8)
    block = length_z * rows // owners
    dims = (spaces, slices, chunks, depth, length_z, rows, width_y, owners, block)

    def pair(length):
        full = jnp.asarray(sine(length), jnp.float32)
        return jnp.stack(split_pair(full))

    sides = jnp.asarray(eigen(width_x)[:, None] + eigen(width_y)[None, :], jnp.float32)
    f32 = jnp.float32
    flat = length_z * rows
    dma = pltpu.SemaphoreType.DMA
    vmem = pl.BlockSpec(memory_space=pltpu.VMEM)
    hbm = pl.BlockSpec(memory_space=pl.ANY)
    return pl.pallas_call(
        functools.partial(kernel, dims),
        out_shape=jax.ShapeDtypeStruct((1, 5, depth, width_x, width_y), f32),
        in_specs=[pl.BlockSpec(memory_space=pltpu.SMEM), hbm, hbm, hbm, vmem, vmem, vmem],
        out_specs=hbm,
        scratch_shapes=[
            pltpu.VMEM((depth, width_x, width_y), f32),
            pltpu.VMEM((depth, width_x, width_y), f32),
            pltpu.VMEM((5, depth, width_x, width_y), f32),
            pltpu.VMEM((5, depth, width_x, width_y), f32),
            pltpu.VMEM((chunks, spaces, 6, depth, rows, width_y), f32),
            pltpu.VMEM((chunks, spaces, 6, depth, rows, width_y), f32),
            pltpu.VMEM((chunks, flat, width_y), f32),
            pltpu.VMEM((chunks, flat, width_y), f32),
            pltpu.VMEM((chunks, flat, width_y), f32),
            pltpu.VMEM((8, width_y), f32),
            pltpu.VMEM((slices, 8, width_y), f32),
            pltpu.VMEM((chunks, 4, flat, width_y), f32),
            pltpu.VMEM((chunks, 4, flat, width_y), f32),
            pltpu.VMEM((chunks, 4, flat, width_y), f32),
            pltpu.VMEM((chunks, owners, 2, block, width_y), f32),
            pltpu.VMEM((chunks, slices, 2, block, width_y), f32),
            pltpu.VMEM((chunks, slices, block, width_y), f32),
            pltpu.VMEM((chunks, slices, block, width_y), f32),
            pltpu.VMEM((chunks, slices, 2, block, width_y), f32),
            pltpu.VMEM((chunks, owners, 2, block, width_y), f32),
            pltpu.VMEM((chunks, spaces, 5, depth, rows, width_y), f32),
            pltpu.VMEM((chunks, spaces, 5, depth, rows, width_y), f32),
            dma((3,)),
            dma((5,)),
            dma((chunks, 3, spaces)),
            dma((chunks, 3, spaces)),
            dma((chunks,)),
            dma((chunks,)),
            dma((slices,)),
            dma((slices,)),
            dma((chunks, owners)),
            dma((chunks, slices)),
            dma((chunks, slices)),
            dma((chunks, owners)),
            dma((chunks, 5, spaces)),
            dma((chunks, 5, spaces)),
        ],
        compiler_params=pltpu.CompilerParams(collective_id=0, has_side_effects=True),
    )(step_size, initial, start_guess, forcing, pair(width_x), pair(width_y), sides)


def solution(mesh):
    in_specs = (
        P("space", None, None),
        P("tm", "space", None, None),
        P("tm", None, "space", None, None),
        P("tm"),
    )
    out_specs = P("tm", None, "space", None, None)
    return jax.shard_map(body, mesh=mesh, in_specs=in_specs, out_specs=out_specs, check_vma=False)
```

time: 295 us -> 41 us (0.14)
  the two profiles are of different devices: /device:TPU:30 before, /device:TPU:0 now
where the time goes in v1:
time: 41 us; the launch traced here: 40.8 us
  Pallas kernels  38.1 us (93%)
  local copies, waits for them, and re-layouts  1.97 us (5%)
  between operations  0.66 us (2%)
    pallas_call x1, Pallas kernels, body(): pl.pallas_call(functools.partial(kernel, dims), out_shape=jax.ShapeDtypeS...  38.1 us
    unnamed x1, local copies, waits for them, and re-layouts  1.97 us

profile of v1, /device:TPU:0, one launch (start us, length us, event | category | flops | bytes accessed | tf_op | source)
XLA Modules:
  0.0 40.8 jit_solution(2189497251544026474)
XLA Ops:
  0.7 38.1 %shard_map.73 = f32[1,5,2,128,128]{4,3,2,1,0:T(8,128)} custom-call(f32[1]{0:T(128)S(6)} %copy.9.step_ref, f32[2,128,128]{2,1,0:T(8,128)} %initial_hbm.1, f32[1,2,128,128]{3,2,1,0:T(8,128)} %guess_hbm.1, f32[1,5,2,128,128]{4,3,2,1,0:T(8,128)} %forcing_hbm.1, bf16[2,128,128]{2,1,0:T(8,128)(2,1)} %constant.16.x_ref.y_ref, ...), custom_call_target="tpu_custom_call" | custom-call | tf_op jit(solution)/shard_map/pallas_call | solution.py:545
  38.8 2.0 %copy.10 = f32[1,5,2,128,128]{4,3,2,1,0:T(8,128)} copy(f32[1,5,2,128,128]{4,3,2,1,0:T(8,128)} %shard_map.73) | data formatting | bytes 1310720

commit v2 on v1

--- a/solution.py
+++ b/solution.py
@@ -185,13 +185,13 @@
 
 def kernel(
     dims,
-    step_ref, initial_hbm, guess_hbm, forcing_hbm, x_ref, y_ref, lateral_ref,
-    out_hbm,
-    initial, guess, forcing, result,
+    step_ref, initial_hbm, guess_hbm, forcing_hbm, x_hbm, y_hbm, lateral_hbm,
+    result_ref,
+    initial, guess, forcing, x_ref, y_ref, lateral_ref,
     in_send, in_recv, ghat, hhat, ell, own_step, steps,
     gain_c, gain_d, part_b, z_send, z_recv, own_gain, own_cross, r_send, r_recv,
     o_send, o_recv,
-    load_sem, store_sem, in_ss, in_rs, h_ss, h_rs, s_ss, s_rs, z_ss, z_rs, r_ss, r_rs, o_ss, o_rs,
+    load_sem, in_ss, in_rs, h_ss, h_rs, s_ss, s_rs, z_ss, z_rs, r_ss, r_rs, o_ss, o_rs,
 ):
     spaces, slices, chunks, depth, length_z, rows, width_y, owners, block = dims
     me = lax.axis_index("space")
@@ -199,13 +199,6 @@
     _, integrals, _ = TABLES
     width_x = spaces * chunks * rows
 
-    load_guess = pltpu.make_async_copy(guess_hbm.at[0], guess, load_sem.at[0])
-    load_forcing = pltpu.make_async_copy(forcing_hbm.at[0], forcing, load_sem.at[1])
-    load_initial = pltpu.make_async_copy(initial_hbm, initial, load_sem.at[2])
-    load_guess.start()
-    load_forcing.start()
-    load_initial.start()
-
     barrier = pltpu.get_barrier_semaphore()
     for i in range(1, spaces):
         pl.semaphore_signal(
@@ -220,9 +213,18 @@
 
     lax.fori_loop(1, slices, greet, 0)
 
+    sources = (guess_hbm.at[0], x_hbm, y_hbm, forcing_hbm.at[0], initial_hbm, lateral_hbm)
+    loads = [
+        pltpu.make_async_copy(source, target, load_sem.at[i])
+        for i, (source, target) in enumerate(
+            zip(sources, (guess, x_ref, y_ref, forcing, initial, lateral_ref))
+        )
+    ]
+    for load in loads:
+        load.start()
+    load_guess, load_x, load_y, load_forcing, load_initial, load_lateral = loads
+
     step = step_ref[0]
-    x_pair = (x_ref[0], x_ref[1])
-    y_pair = (y_ref[0], y_ref[1])
     own_step[...] = jnp.full(own_step.shape, step, jnp.float32)
     steps[place] = jnp.full(own_step.shape, step, jnp.float32)
 
@@ -260,6 +262,10 @@
             in_copy(c, group, peer, peer).wait_recv()
 
     load_guess.wait()
+    load_x.wait()
+    load_y.wait()
+    x_pair = (x_ref[0], x_ref[1])
+    y_pair = (y_ref[0], y_ref[1])
     put(guess[...], 0)
     pl.semaphore_wait(barrier, spaces - 1 + slices - 1)
     for c in range(chunks):
@@ -286,12 +292,6 @@
 
     for c in range(chunks):
         keep(c, 0, 1)
-    load_forcing.wait()
-    for m in range(4):
-        put(step * weighted(integrals[m], [forcing[j] for j in range(5)]), m + 1)
-    for c in range(chunks):
-        in_start(c, 1)
-        keep(c, 1, 5)
     load_initial.wait()
 
     @pl.when(place == 0)
@@ -301,7 +301,14 @@
             in_start(c, 2)
             keep(c, 5, 6)
 
+    load_forcing.wait()
+    for m in range(4):
+        put(step * weighted(integrals[m], [forcing[j] for j in range(5)]), m + 1)
+    for c in range(chunks):
+        in_start(c, 1)
+        keep(c, 1, 5)
     z_eigen = eigen(length_z)
+    load_lateral.wait()
     for c in range(chunks):
         low = pl.multiple_of((me * chunks + c) * rows, 8)
         base = lateral_ref[pl.ds(low, rows), :]
@@ -444,12 +451,16 @@
             peers(lambda peer: r_copy(c, peer, place).start())
             r_recv[c, place] = r_send[c, place]
 
-    def o_copy(c, m, peer, source):
+    def o_groups(c):
+        return ((0, 1), (1, 2), (2, 3), (3, 4), (4, 5)) if c == chunks - 1 else ((0, 5),)
+
+    def o_copy(c, group, peer, source):
+        low, high = o_groups(c)[group]
         return pltpu.make_async_remote_copy(
-            src_ref=o_send.at[c, peer, m],
-            dst_ref=o_recv.at[c, source, m],
-            send_sem=o_ss.at[c, m, peer],
-            recv_sem=o_rs.at[c, m, source],
+            src_ref=o_send.at[c, peer, low:high],
+            dst_ref=o_recv.at[c, source, low:high],
+            send_sem=o_ss.at[c, group, peer],
+            recv_sem=o_rs.at[c, group, source],
             device_id={"space": peer},
             device_id_type=MESH,
         )
@@ -469,18 +480,19 @@
             planes = z_sine([value[k * rows : (k + 1) * rows] for k in range(length_z)])
             for z in range(length_z):
                 o_send[c, z // depth, m, z % depth] = planes[z]
-            for i in range(1, spaces):
-                o_copy(c, m, lax.rem(me + i, spaces), me).start()
             o_recv[c, me, m] = o_send[c, me, m]
-
-    def store(m):
-        return pltpu.make_async_copy(result.at[m], out_hbm.at[0, m], store_sem.at[m])
+            for group, (_, high) in enumerate(o_groups(c)):
+                if high == m + 1:
+                    for i in range(1, spaces):
+                        o_copy(c, group, lax.rem(me + i, spaces), me).start()
 
     for m in range(5):
         for c in range(chunks):
-            for i in range(1, spaces):
-                peer = lax.rem(me + i, spaces)
-                o_copy(c, m, peer, peer).wait_recv()
+            for group, (low, _) in enumerate(o_groups(c)):
+                if low == m:
+                    for i in range(1, spaces):
+                        peer = lax.rem(me + i, spaces)
+                        o_copy(c, group, peer, peer).wait_recv()
         field = jnp.stack(
             [
                 jnp.concatenate(
@@ -491,16 +503,15 @@
         )
         planes = lateral(field, x_pair, y_pair)
         for z in range(depth):
-            result[m, z] = planes[z]
-        store(m).start()
+            result_ref[0, m, z] = planes[z]
 
     for c in range(chunks):
         for i in range(1, spaces):
             peer = lax.rem(me + i, spaces)
             in_copy(c, 0, peer, me).wait_send()
             in_copy(c, 1, peer, me).wait_send()
-            for m in range(5):
-                o_copy(c, m, peer, me).wait_send()
+            for group in range(len(o_groups(c))):
+                o_copy(c, group, peer, me).wait_send()
 
         @pl.when(place == 0)
         def _():
@@ -518,8 +529,6 @@
             peers(lambda peer: r_copy(c, peer, place).wait_send())
 
     peers(lambda peer: step_copy(peer, place).wait_send())
-    for m in range(5):
-        store(m).wait()
 
 
 def body(initial, start_guess, forcing, step_size):
@@ -544,14 +553,16 @@
     hbm = pl.BlockSpec(memory_space=pl.ANY)
     return pl.pallas_call(
         functools.partial(kernel, dims),
-        out_shape=jax.ShapeDtypeStruct((1, 5, depth, width_x, width_y), f32),
-        in_specs=[pl.BlockSpec(memory_space=pltpu.SMEM), hbm, hbm, hbm, vmem, vmem, vmem],
-        out_specs=hbm,
+        out_shape=pltpu.VMEM((1, 5, depth, width_x, width_y), f32),
+        in_specs=[pl.BlockSpec(memory_space=pltpu.SMEM), hbm, hbm, hbm, hbm, hbm, hbm],
+        out_specs=vmem,
         scratch_shapes=[
             pltpu.VMEM((depth, width_x, width_y), f32),
             pltpu.VMEM((depth, width_x, width_y), f32),
             pltpu.VMEM((5, depth, width_x, width_y), f32),
-            pltpu.VMEM((5, depth, width_x, width_y), f32),
+            pltpu.VMEM((2, width_x, width_x), jnp.bfloat16),
+            pltpu.VMEM((2, width_y, width_y), jnp.bfloat16),
+            pltpu.VMEM((width_x, width_y), f32),
             pltpu.VMEM((chunks, spaces, 6, depth, rows, width_y), f32),
             pltpu.VMEM((chunks, spaces, 6, depth, rows, width_y), f32),
             pltpu.VMEM((chunks, flat, width_y), f32),
@@ -570,8 +581,7 @@
             pltpu.VMEM((chunks, owners, 2, block, width_y), f32),
             pltpu.VMEM((chunks, spaces, 5, depth, rows, width_y), f32),
             pltpu.VMEM((chunks, spaces, 5, depth, rows, width_y), f32),
-            dma((3,)),
-            dma((5,)),
+            dma((6,)),
             dma((chunks, 3, spaces)),
             dma((chunks, 3, spaces)),
             dma((chunks,)),

time: 41 us -> 36.5 us (0.89)
  Pallas kernels: 38.1 us -> 34.9 us
  local copies, waits for them, and re-layouts: 1.97 us -> 0.84 us
    pallas_call x1, Pallas kernels: 38.1 us -> 34.9 us  [body(): pl.pallas_call(functools.partial(kernel, dims), out_shape=pltpu.VMEM((1,...]
    unnamed x1, local copies, waits for them, and re-layouts: 1.97 us -> 0.84 us
where the time goes in v2:
time: 36.5 us; the launch traced here: 36.4 us
  Pallas kernels  34.9 us (96%)
  local copies, waits for them, and re-layouts  0.84 us (2%)
  between operations  0.66 us (2%)
    pallas_call x1, Pallas kernels, body(): pl.pallas_call(functools.partial(kernel, dims), out_shape=pltpu.VMEM((1,...  34.9 us
    unnamed x1, local copies, waits for them, and re-layouts  0.84 us

profile of v2, /device:TPU:0, one launch (start us, length us, event | category | flops | bytes accessed | tf_op | source)
XLA Modules:
  0.0 36.4 jit_solution(14889153627874337634)
XLA Ops:
  0.7 34.9 %shard_map.73 = f32[1,5,2,128,128]{4,3,2,1,0:T(8,128)S(1)} custom-call(f32[1]{0:T(128)S(6)} %copy.10.step_ref, f32[2,128,128]{2,1,0:T(8,128)} %initial_hbm.1, f32[1,2,128,128]{3,2,1,0:T(8,128)} %guess_hbm.1, f32[1,5,2,128,128]{4,3,2,1,0:T(8,128)} %forcing_hbm.1, bf16[2,128,128]{2,1,0:T(8,128)(2,1)} %constant.16.x_hbm.y_hbm, ...), custom_call_target="tpu_custom_call" | custom-call | tf_op jit(solution)/shard_map/pallas_call | solution.py:554
  35.5 0.8 %copy.9 = f32[1,5,2,128,128]{4,3,2,1,0:T(8,128)} copy(f32[1,5,2,128,128]{4,3,2,1,0:T(8,128)S(1)} %shard_map.73) | data formatting | bytes 1310720

commit v3 on v2

--- a/solution.py
+++ b/solution.py
@@ -286,7 +286,11 @@
             action(lax.rem(place + i, slices))
             return carry
 
-        lax.fori_loop(1, slices, one, 0)
+        if slices > 8:
+            lax.fori_loop(1, slices, one, 0)
+        else:
+            for i in range(1, slices):
+                one(i, 0)
 
     peers(lambda peer: step_copy(peer, place).start())
 
@@ -324,7 +328,7 @@
                 gain_d[c, m - 1, at] = crossed[m]
         return carry
 
-    lax.fori_loop(0, length_z, table, 0)
+    lax.fori_loop(0, length_z, table, 0, unroll=2)
 
     def planes_of(c, slot):
         return [in_recv[c, z // depth, slot, z % depth] for z in range(length_z)]
@@ -361,14 +365,14 @@
                 own_cross[c, p] = crossed[4]
             return carry
 
-        lax.fori_loop(0, slices, one, 0)
+        lax.fori_loop(0, slices, one, 0, unroll=2)
 
     def z_copy(c, owner, source):
         return pltpu.make_async_remote_copy(
             src_ref=z_send.at[c, owner],
             dst_ref=z_recv.at[c, source],
-            send_sem=z_ss.at[c, owner],
-            recv_sem=z_rs.at[c, source],
+            send_sem=z_ss.at[c],
+            recv_sem=z_rs.at[c],
             device_id={"tm": owner},
             device_id_type=MESH,
         )
@@ -378,6 +382,16 @@
             action()
         else:
             pl.when(owner < owners)(action)
+
+    def bulk_wait(ref, sem, count):
+        pltpu.make_async_copy(ref.at[0:count], ref.at[0:count], sem).wait()
+
+    def owner_wait(ref, sem):
+        if owners == slices:
+            bulk_wait(ref, sem, owners - 1)
+        else:
+            pl.when(place < owners)(lambda: bulk_wait(ref, sem, owners - 1))
+            pl.when(place >= owners)(lambda: bulk_wait(ref, sem, owners))
 
     first = jnp.where(place == 0, 1.0, 0.0).astype(jnp.float32)
     for c in range(chunks):
@@ -414,7 +428,7 @@
             z_send[c, i, 1] = rest[4] + (gain + cross) * seen
             return carry
 
-        lax.fori_loop(0, owners, solve, 0)
+        lax.fori_loop(0, owners, solve, 0, unroll=4)
         peers(lambda peer: to_owner(peer, lambda: z_copy(c, peer, place).start()))
 
         @pl.when(place < owners)
@@ -425,8 +439,8 @@
         return pltpu.make_async_remote_copy(
             src_ref=r_send.at[c, target],
             dst_ref=r_recv.at[c, owner],
-            send_sem=r_ss.at[c, target],
-            recv_sem=r_rs.at[c, owner],
+            send_sem=r_ss.at[c],
+            recv_sem=r_rs.at[c],
             device_id={"tm": target},
             device_id_type=MESH,
         )
@@ -434,7 +448,7 @@
     for c in range(chunks):
         @pl.when(place < owners)
         def _():
-            peers(lambda peer: z_copy(c, peer, peer).wait_recv())
+            bulk_wait(z_recv.at[c], z_rs.at[c], slices - 1)
 
             def scan(p, state):
                 lower, upper = state
@@ -447,12 +461,12 @@
                 )
 
             zero = jnp.zeros((block, width_y), jnp.float32)
-            lax.fori_loop(0, slices, scan, (zero, zero))
+            lax.fori_loop(0, slices, scan, (zero, zero), unroll=8)
             peers(lambda peer: r_copy(c, peer, place).start())
             r_recv[c, place] = r_send[c, place]
 
     def o_groups(c):
-        return ((0, 1), (1, 2), (2, 3), (3, 4), (4, 5)) if c == chunks - 1 else ((0, 5),)
+        return ((0, 3), (3, 5)) if c == chunks - 1 else ((0, 5),)
 
     def o_copy(c, group, peer, source):
         low, high = o_groups(c)[group]
@@ -466,7 +480,7 @@
         )
 
     for c in range(chunks):
-        peers(lambda peer: to_owner(peer, lambda: r_copy(c, peer, peer).wait_recv()))
+        owner_wait(r_recv.at[c], r_rs.at[c])
         own = hhat[c].reshape(owners, block, width_y)
         lower = jnp.where(place == 0, own, r_recv[c, :, 0]).reshape(length_z * rows, width_y)
         upper = jnp.where(place == 0, own, r_recv[c, :, 1]).reshape(length_z * rows, width_y)
@@ -486,6 +500,29 @@
                     for i in range(1, spaces):
                         o_copy(c, group, lax.rem(me + i, spaces), me).start()
 
+    for c in range(chunks):
+        for i in range(1, spaces):
+            peer = lax.rem(me + i, spaces)
+            in_copy(c, 0, peer, me).wait_send()
+            in_copy(c, 1, peer, me).wait_send()
+
+        @pl.when(place == 0)
+        def _():
+            for i in range(1, spaces):
+                in_copy(c, 2, lax.rem(me + i, spaces), me).wait_send()
+
+        @pl.when(place < slices - 1)
+        def _():
+            h_copy(c, after).wait_send()
+
+        owner_wait(z_send.at[c], z_ss.at[c])
+
+        @pl.when(place < owners)
+        def _():
+            bulk_wait(r_send.at[c], r_ss.at[c], slices - 1)
+
+    peers(lambda peer: step_copy(peer, place).wait_send())
+
     for m in range(5):
         for c in range(chunks):
             for group, (low, _) in enumerate(o_groups(c)):
@@ -507,28 +544,8 @@
 
     for c in range(chunks):
         for i in range(1, spaces):
-            peer = lax.rem(me + i, spaces)
-            in_copy(c, 0, peer, me).wait_send()
-            in_copy(c, 1, peer, me).wait_send()
             for group in range(len(o_groups(c))):
-                o_copy(c, group, peer, me).wait_send()
-
-        @pl.when(place == 0)
-        def _():
-            for i in range(1, spaces):
-                in_copy(c, 2, lax.rem(me + i, spaces), me).wait_send()
-
-        @pl.when(place < slices - 1)
-        def _():
-            h_copy(c, after).wait_send()
-
-        peers(lambda peer: to_owner(peer, lambda: z_copy(c, peer, place).wait_send()))
-
-        @pl.when(place < owners)
-        def _():
-            peers(lambda peer: r_copy(c, peer, place).wait_send())
-
-    peers(lambda peer: step_copy(peer, place).wait_send())
+                o_copy(c, group, lax.rem(me + i, spaces), me).wait_send()
 
 
 def body(initial, start_guess, forcing, step_size):
@@ -588,10 +605,10 @@
             dma((chunks,)),
             dma((slices,)),
             dma((slices,)),
-            dma((chunks, owners)),
-            dma((chunks, slices)),
-            dma((chunks, slices)),
-            dma((chunks, owners)),
+            dma((chunks,)),
+            dma((chunks,)),
+            dma((chunks,)),
+            dma((chunks,)),
             dma((chunks, 5, spaces)),
             dma((chunks, 5, spaces)),
         ],

time: 36.5 us -> 34.9 us (0.956)
  Pallas kernels: 34.9 us -> 33.2 us
    pallas_call x1, Pallas kernels: 34.9 us -> 33.2 us  [body(): pl.pallas_call(functools.partial(kernel, dims), out_shape=pltpu.VMEM((1,...]
where the time goes in v3:
time: 34.9 us; the launch traced here: 34.7 us
  Pallas kernels  33.2 us (95%)
  local copies, waits for them, and re-layouts  0.84 us (2%)
  between operations  0.66 us (2%)
    pallas_call x1, Pallas kernels, body(): pl.pallas_call(functools.partial(kernel, dims), out_shape=pltpu.VMEM((1,...  33.2 us
    unnamed x1, local copies, waits for them, and re-layouts  0.84 us

profile of v3, /device:TPU:0, one launch (start us, length us, event | category | flops | bytes accessed | tf_op | source)
XLA Modules:
  0.0 34.7 jit_solution(7797079307704597269)
XLA Ops:
  0.7 33.2 %shard_map.73 = f32[1,5,2,128,128]{4,3,2,1,0:T(8,128)S(1)} custom-call(f32[1]{0:T(128)S(6)} %copy.10.step_ref, f32[2,128,128]{2,1,0:T(8,128)} %initial_hbm.1, f32[1,2,128,128]{3,2,1,0:T(8,128)} %guess_hbm.1, f32[1,5,2,128,128]{4,3,2,1,0:T(8,128)} %forcing_hbm.1, bf16[2,128,128]{2,1,0:T(8,128)(2,1)} %constant.16.x_hbm.y_hbm, ...), custom_call_target="tpu_custom_call" | custom-call | tf_op jit(solution)/shard_map/pallas_call | solution.py:571
  33.9 0.8 %copy.9 = f32[1,5,2,128,128]{4,3,2,1,0:T(8,128)} copy(f32[1,5,2,128,128]{4,3,2,1,0:T(8,128)S(1)} %shard_map.73) | data formatting | bytes 1310720

commit v4 on v3

--- a/solution.py
+++ b/solution.py
@@ -292,7 +292,6 @@
             for i in range(1, slices):
                 one(i, 0)
 
-    peers(lambda peer: step_copy(peer, place).start())
 
     for c in range(chunks):
         keep(c, 0, 1)
@@ -311,6 +310,8 @@
     for c in range(chunks):
         in_start(c, 1)
         keep(c, 1, 5)
+    peers(lambda peer: step_copy(peer, place).start())
+
     z_eigen = eigen(length_z)
     load_lateral.wait()
     for c in range(chunks):
@@ -494,11 +495,11 @@
             planes = z_sine([value[k * rows : (k + 1) * rows] for k in range(length_z)])
             for z in range(length_z):
                 o_send[c, z // depth, m, z % depth] = planes[z]
-            o_recv[c, me, m] = o_send[c, me, m]
             for group, (_, high) in enumerate(o_groups(c)):
                 if high == m + 1:
                     for i in range(1, spaces):
                         o_copy(c, group, lax.rem(me + i, spaces), me).start()
+            o_recv[c, me, m] = o_send[c, me, m]
 
     for c in range(chunks):
         for i in range(1, spaces):

time: 34.9 us -> 34.9 us (level)
  no operation moved by 1% of the time
where the time goes in v4:
time: 34.9 us; the launch traced here: 34.7 us
  Pallas kernels  33.2 us (95%)
  local copies, waits for them, and re-layouts  0.84 us (2%)
  between operations  0.66 us (2%)
    pallas_call x1, Pallas kernels, body(): pl.pallas_call(functools.partial(kernel, dims), out_shape=pltpu.VMEM((1,...  33.2 us
    unnamed x1, local copies, waits for them, and re-layouts  0.84 us

profile of v4, /device:TPU:0, one launch (start us, length us, event | category | flops | bytes accessed | tf_op | source)
XLA Modules:
  0.0 34.7 jit_solution(4531539238493525374)
XLA Ops:
  0.7 33.2 %shard_map.73 = f32[1,5,2,128,128]{4,3,2,1,0:T(8,128)S(1)} custom-call(f32[1]{0:T(128)S(6)} %copy.10.step_ref, f32[2,128,128]{2,1,0:T(8,128)} %initial_hbm.1, f32[1,2,128,128]{3,2,1,0:T(8,128)} %guess_hbm.1, f32[1,5,2,128,128]{4,3,2,1,0:T(8,128)} %forcing_hbm.1, bf16[2,128,128]{2,1,0:T(8,128)(2,1)} %constant.16.x_hbm.y_hbm, ...), custom_call_target="tpu_custom_call" | custom-call | tf_op jit(solution)/shard_map/pallas_call | solution.py:572
  33.9 0.8 %copy.9 = f32[1,5,2,128,128]{4,3,2,1,0:T(8,128)} copy(f32[1,5,2,128,128]{4,3,2,1,0:T(8,128)S(1)} %shard_map.73) | data formatting | bytes 1310720
